TPU v7x, 32 devices: a whole 2x2x4 slice. The times are simulated.
32 devices in a mesh: dp: 2 (over x), fsdp: 16 (over z, y, core).
Axes of the slice: x: 2, y: 2, z: 4, core: 2. Of those that a mesh axis runs over, the one named last changes fastest.
Arguments:
- byte_ids: int32 [2, 2048], P('dp', 'fsdp'), may hold values from 0 to 255
- cotangent: bfloat16 [2, 2048, 1024], P('dp', 'fsdp'), may hold values from -6 to 6
- patch_table: bfloat16 [2048, 128], P('fsdp'), may hold values from -6 to 6
- global_gain: bfloat16 [1024], P('fsdp'), may hold values from 0.099609375 to 1.8984375
- in_proj: bfloat16 [1024, 4384], P('fsdp'), may hold values from -0.1875 to 0.1875
- conv_weight: bfloat16 [2304, 4], P('fsdp'), may hold values from -3 to 3
- conv_bias: bfloat16 [2304], P('fsdp'), may hold values from -0.5 to 0.5
- step_bias: bfloat16 [32], P('fsdp'), may hold values from -7 to -3
- decay_log: bfloat16 [32], P('fsdp'), may hold values from -1 to 1
- skip_gain: bfloat16 [32], P('fsdp'), may hold values from 0.5 to 1.5
- mixer_gain: bfloat16 [2048], P('fsdp'), may hold values from 0.099609375 to 1.8984375
- out_proj: bfloat16 [2048, 1024], P('fsdp'), may hold values from -0.125 to 0.125
- byte_table: bfloat16 [256, 1024], P('fsdp'), may hold values from -6 to 6
- local_gain: bfloat16 [1024], P('fsdp'), may hold values from 0.099609375 to 1.8984375
- qkv_proj: bfloat16 [1024, 3072], P('fsdp'), may hold values from -0.1875 to 0.1875
- attn_out: bfloat16 [1024, 1024], P('fsdp'), may hold values from -0.375 to 0.375
- ffn_gain: bfloat16 [1024], P('fsdp'), may hold values from 0.099609375 to 1.8984375
- gate_up: bfloat16 [1024, 8192], P('fsdp'), may hold values from -0.1875 to 0.1875
- down_proj: bfloat16 [4096, 1024], P('fsdp'), may hold values from -0.125 to 0.125
Outputs:
- activations: bfloat16 [2, 2048, 1024], P('dp', 'fsdp')
- patch_table_grad: float32 [2048, 128], P('fsdp')
- global_gain_grad: float32 [1024], P('fsdp')
- in_proj_grad: float32 [1024, 4384], P('fsdp')
- conv_weight_grad: float32 [2304, 4], P('fsdp')
- conv_bias_grad: float32 [2304], P('fsdp')
- step_bias_grad: float32 [32], P('fsdp')
- decay_log_grad: float32 [32], P('fsdp')
- skip_gain_grad: float32 [32], P('fsdp')
- mixer_gain_grad: float32 [2048], P('fsdp')
- out_proj_grad: float32 [2048, 1024], P('fsdp')
- byte_table_grad: float32 [256, 1024], P('fsdp')
- local_gain_grad: float32 [1024], P('fsdp')
- qkv_proj_grad: float32 [1024, 3072], P('fsdp')
- attn_out_grad: float32 [1024, 1024], P('fsdp')
- ffn_gain_grad: float32 [1024], P('fsdp')
- gate_up_grad: float32 [1024, 8192], P('fsdp')
- down_proj_grad: float32 [4096, 1024], P('fsdp')
All inputs are finite; a program needn't handle non-finite values.
Results may differ from a plain program's by a relative error of at most 0.03.
Values may be sent and summed in bfloat16 or wider, within the bound.
A program may use at most 320 MiB of HBM per device.

v0:
```python
import jax
import jax.numpy as jnp
from jax import lax
from jax.sharding import PartitionSpec as P

D = 1024
NST = 128
HM = 32
HA = 16
FF = 4096
VOCAB = 256
KC = 4
PATCH = 8
DI = 2048
PM = 64
DA = 64
DG = 128
XBC = 2304
INW = 4384


highest = lax.Precision.HIGHEST
epsilon = 1e-05


def from_behind(block, axis, distance):
    devices = range(lax.axis_size(axis))
    route = [(i - distance, i) for i in devices if i - distance in devices]
    return lax.ppermute(block, axis, route)


def entering(shard, axis, join, neutral):
    place = lax.axis_index(axis)
    gathered = jax.tree.map(
        lambda a, kind: lax.all_gather(a.astype(kind), axis), shard, (jnp.bfloat16, jnp.bfloat16)
    )
    state = jax.tree.map(lambda a, e: jnp.zeros_like(a) + jnp.asarray(e, a.dtype), shard, neutral)

    def one(hop, state):
        return join(
            state,
            jax.tree.map(
                lambda a, own: lax.dynamic_index_in_dim(a, hop, 0, False).astype(own.dtype),
                gathered,
                shard,
            ),
        )

    return lax.fori_loop(0, place, one, state)


def entering_2(shard, axis, combine, identity):
    size, index = (lax.axis_size(axis), lax.axis_index(axis))
    everything = jax.tree.map(
        lambda part, kind: lax.all_gather(part.astype(kind), axis),
        shard,
        jax.tree.map(lambda a: jnp.bfloat16 if a.dtype == jnp.float32 else a.dtype, shard),
    )
    start = jax.tree.map(
        lambda part, zero: jnp.broadcast_to(jnp.asarray(zero, part.dtype), part.shape),
        shard,
        identity,
    )

    def hop(k, before):
        at = size - 1 - k
        reached = at > index
        new = combine(
            before, jax.tree.map(lambda part, own: part[at].astype(own.dtype), everything, shard)
        )
        return jax.tree.map(lambda a, b: jnp.where(reached, a, b), new, before)

    return lax.fori_loop(0, size, hop, start)


def scale_rows(values, scale_gain):
    return (
        values * lax.rsqrt(jnp.mean(values * values, axis=-1, keepdims=True) + epsilon) * scale_gain
    )


def state_blocks(inputs, b_rows, c_rows, step_size, decay_rate, skip_gain):
    cumulative = jnp.cumsum(step_size * decay_rate, axis=1)
    length = inputs.shape[1]
    causal = (jnp.arange(length)[None, :] <= jnp.arange(length)[:, None])[None, :, :, None]
    spread = cumulative[:, :, None, :] - cumulative[:, None, :, :]
    weights = jnp.exp(jnp.where(causal, spread, -jnp.inf))
    intersection = jnp.einsum("btn,bun->btu", c_rows, b_rows, precision=highest)
    scaled = inputs * step_size[..., None]
    local_out = jnp.einsum(
        "btuh,buhp->bthp", intersection[..., None] * weights, scaled, precision=highest
    )
    local_out = local_out + skip_gain[:, None] * inputs
    tail_decay = jnp.exp(cumulative[:, -1:, :] - cumulative)
    summary = jnp.einsum("buh,buhp,bun->bhpn", tail_decay, scaled, b_rows, precision=highest)
    return (local_out, cumulative, summary, jnp.exp(cumulative[:, -1, :]))


def state_join(local_out, c_rows, cumulative, state_in):
    carried = jnp.einsum("btn,bhpn->bthp", c_rows, state_in, precision=highest)
    return local_out + carried * jnp.exp(cumulative)[..., None]


def patch_attention(qkv_rows):
    patches = qkv_rows.shape[0] // PATCH
    pieces = qkv_rows.reshape(patches, PATCH, 3, HA, DA)
    scores = jnp.einsum(
        "pihd,pjhd->phij", pieces[:, :, 0], pieces[:, :, 1], precision=highest
    ) * DA ** (-0.5)
    causal = jnp.arange(PATCH)[None, :] <= jnp.arange(PATCH)[:, None]
    scores = jnp.where(causal, scores, -1e30)
    attention_weights = jax.nn.softmax(scores, axis=-1)
    combined = jnp.einsum("phij,pjhd->pihd", attention_weights, pieces[:, :, 2], precision=highest)
    return combined.reshape(patches * PATCH, HA * DA)


def mixer_front(
    conv_input, conv_rim, conv_weight, conv_bias, step_raw, step_bias, decay_log, skip_gain
):
    groups = conv_input.shape[0]
    length = conv_input.shape[1]
    padded = jnp.concatenate([conv_rim, conv_input], 1)
    summed = conv_bias
    for offset in range(KC):
        summed = summed + padded[:, offset : offset + length] * conv_weight[:, offset]
    conv_out = jax.nn.silu(summed)
    inputs = conv_out[..., :DI].reshape(groups, length, HM, PM)
    b_rows = conv_out[..., DI : DI + NST]
    c_rows = conv_out[..., DI + NST :]
    step_size = jax.nn.softplus(step_raw + step_bias)
    local_out, cumulative, summary, decay_total = state_blocks(
        inputs, b_rows, c_rows, step_size, -jnp.exp(decay_log), skip_gain
    )
    return (local_out, c_rows, cumulative, summary, decay_total)


def mixer_back(local_out, c_rows, cumulative, state_in, gate_z, mixer_gain):
    joined = state_join(local_out, c_rows, cumulative, state_in)
    groups = joined.shape[0]
    length = joined.shape[1]
    return scale_rows(joined.reshape(groups, length, DI) * jax.nn.silu(gate_z), mixer_gain)


def gate_product(gate_vals):
    return jax.nn.silu(gate_vals[:, :FF]) * gate_vals[:, FF:]


def chain_states(earlier, later_part):
    return (earlier[0] * later_part[0], later_part[0][..., None, None] * earlier[1] + later_part[1])


def times_transposed(grad_rows, matrix):
    return lax.dot_general(
        grad_rows, matrix, (((1,), (1,)), ((), ())), preferred_element_type=jnp.float32
    )


def outer_rows(left_rows, grad_rows):
    return lax.dot_general(
        left_rows, grad_rows, (((0,), (0,)), ((), ())), preferred_element_type=jnp.float32
    )


def on_device(
    byte_ids,
    cotangent,
    patch_table,
    global_gain,
    in_proj,
    conv_weight,
    conv_bias,
    step_bias,
    decay_log,
    skip_gain,
    mixer_gain,
    out_proj,
    byte_table,
    local_gain,
    qkv_proj,
    attn_out,
    ffn_gain,
    gate_up,
    down_proj,
):
    groups, length = byte_ids.shape
    patches = length // PATCH
    row_count = groups * length
    patch_grid = byte_ids.reshape(groups, patches, PATCH)
    before = from_behind(patch_grid[:, patches - 1], "fsdp", 1)
    earlier = jnp.concatenate([before[:, None], patch_grid[:, :-1]], 1)
    at_start = jnp.logical_and(jnp.arange(patches) == 0, lax.axis_index("fsdp") == 0)
    keep_row = jnp.where(at_start, 0.0, 1.0).astype(jnp.float32)[None, :, None]
    patch_hot = (earlier[..., None] == jnp.arange(VOCAB, dtype=jnp.int32)).astype(jnp.bfloat16)
    global_set = (
        lax.all_gather(patch_table, "fsdp", axis=0, tiled=True),
        lax.all_gather(global_gain, "fsdp", axis=0, tiled=True),
        lax.all_gather(in_proj, "fsdp", axis=0, tiled=True),
        lax.all_gather(conv_weight, "fsdp", axis=0, tiled=True),
        lax.all_gather(conv_bias, "fsdp", axis=0, tiled=True),
        lax.all_gather(step_bias, "fsdp", axis=0, tiled=True),
        lax.all_gather(decay_log, "fsdp", axis=0, tiled=True),
        lax.all_gather(skip_gain, "fsdp", axis=0, tiled=True),
        lax.all_gather(mixer_gain, "fsdp", axis=0, tiled=True),
        lax.all_gather(out_proj, "fsdp", axis=0, tiled=True),
    )
    global_scale = global_set[1].astype(jnp.float32)
    conv_full = global_set[3].astype(jnp.float32)
    bias_full = global_set[4].astype(jnp.float32)
    step_full = global_set[5].astype(jnp.float32)
    decay_full = global_set[6].astype(jnp.float32)
    skip_full = global_set[7].astype(jnp.float32)
    mixer_scale = global_set[8].astype(jnp.float32)
    table_view = global_set[0].reshape(PATCH, VOCAB, DG)
    patch_input = (
        jnp.einsum(
            "bpjv,jvc->bpjc", patch_hot, table_view, preferred_element_type=jnp.float32
        ).reshape(groups, patches, D)
        * keep_row
    )
    global_normed = (
        scale_rows(patch_input, global_scale).reshape(groups * patches, D).astype(jnp.bfloat16)
    )
    projected = jnp.dot(global_normed, global_set[2], preferred_element_type=jnp.float32).reshape(
        groups, patches, INW
    )
    gate_z = projected[..., :DI]
    conv_input = projected[..., DI : DI + XBC]
    step_raw = projected[..., DI + XBC :]
    conv_rim = from_behind(conv_input[:, patches - (KC - 1) :], "fsdp", 1)
    front_args = (
        conv_input,
        conv_rim,
        conv_full,
        bias_full,
        step_raw,
        step_full,
        decay_full,
        skip_full,
    )
    local_out, c_rows, cumulative, summary, decay_total = mixer_front(*front_args)
    identity = (jnp.ones_like(decay_total), jnp.zeros_like(summary))
    carried = entering((decay_total, summary), "fsdp", chain_states, identity)
    state_in = carried[1]
    mixer_norm = mixer_back(local_out, c_rows, cumulative, state_in, gate_z, mixer_scale)
    mixer_low = mixer_norm.reshape(groups * patches, DI).astype(jnp.bfloat16)
    patch_out = patch_input + jnp.dot(
        mixer_low, global_set[9], preferred_element_type=jnp.float32
    ).reshape(groups, patches, D)
    local_set = (
        lax.all_gather(byte_table, "fsdp", axis=0, tiled=True),
        lax.all_gather(local_gain, "fsdp", axis=0, tiled=True),
        lax.all_gather(qkv_proj, "fsdp", axis=0, tiled=True),
        lax.all_gather(attn_out, "fsdp", axis=0, tiled=True),
        lax.all_gather(ffn_gain, "fsdp", axis=0, tiled=True),
        lax.all_gather(gate_up, "fsdp", axis=0, tiled=True),
        lax.all_gather(down_proj, "fsdp", axis=0, tiled=True),
    )
    local_scale = local_set[1].astype(jnp.float32)
    ffn_scale = local_set[4].astype(jnp.float32)
    byte_hot = (
        byte_ids.reshape(row_count)[:, None] == jnp.arange(VOCAB, dtype=jnp.int32)[None, :]
    ).astype(jnp.bfloat16)
    spread_out = jnp.broadcast_to(patch_out[:, :, None, :], (groups, patches, PATCH, D)).reshape(
        row_count, D
    )
    stream = jnp.dot(byte_hot, local_set[0], preferred_element_type=jnp.float32) + spread_out
    first_norm = scale_rows(stream, local_scale).astype(jnp.bfloat16)
    qkv_rows = jnp.dot(first_norm, local_set[2], preferred_element_type=jnp.float32)
    attended = patch_attention(qkv_rows).astype(jnp.bfloat16)
    residual = stream + jnp.dot(attended, local_set[3], preferred_element_type=jnp.float32)
    second_norm = scale_rows(residual, ffn_scale).astype(jnp.bfloat16)
    gate_vals = jnp.dot(second_norm, local_set[5], preferred_element_type=jnp.float32)
    hidden = gate_product(gate_vals).astype(jnp.bfloat16)
    final = residual + jnp.dot(hidden, local_set[6], preferred_element_type=jnp.float32)
    activations = final.astype(jnp.bfloat16).reshape(groups, length, D)
    local_set = (
        lax.all_gather(byte_table, "fsdp", axis=0, tiled=True),
        lax.all_gather(local_gain, "fsdp", axis=0, tiled=True),
        lax.all_gather(qkv_proj, "fsdp", axis=0, tiled=True),
        lax.all_gather(attn_out, "fsdp", axis=0, tiled=True),
        lax.all_gather(ffn_gain, "fsdp", axis=0, tiled=True),
        lax.all_gather(gate_up, "fsdp", axis=0, tiled=True),
        lax.all_gather(down_proj, "fsdp", axis=0, tiled=True),
    )
    grad_final = cotangent.reshape(row_count, D)
    grad_down = outer_rows(hidden, grad_final)
    grad_hidden = times_transposed(grad_final, local_set[6])
    _, pull_gate = jax.vjp(gate_product, gate_vals)
    grad_gates = pull_gate(grad_hidden)[0].astype(jnp.bfloat16)
    grad_gate_up = outer_rows(second_norm, grad_gates)
    grad_second = times_transposed(grad_gates, local_set[5])
    _, pull_second = jax.vjp(scale_rows, residual, ffn_scale)
    grad_res_norm, grad_ffn_gain = pull_second(grad_second)
    grad_residual = grad_final.astype(jnp.float32) + grad_res_norm
    residual_low = grad_residual.astype(jnp.bfloat16)
    grad_attn_out = outer_rows(attended, residual_low)
    grad_attended = times_transposed(residual_low, local_set[3])
    _, pull_attention = jax.vjp(patch_attention, qkv_rows)
    grad_qkv_rows = pull_attention(grad_attended)[0].astype(jnp.bfloat16)
    grad_qkv = outer_rows(first_norm, grad_qkv_rows)
    grad_first = times_transposed(grad_qkv_rows, local_set[2])
    _, pull_first = jax.vjp(scale_rows, stream, local_scale)
    grad_stream_norm, grad_local_gain = pull_first(grad_first)
    grad_stream = grad_residual + grad_stream_norm
    grad_byte_table = outer_rows(byte_hot, grad_stream.astype(jnp.bfloat16))
    grad_patch_out = grad_stream.reshape(groups, patches, PATCH, D).sum(axis=2)
    local_terms = (
        grad_byte_table,
        grad_local_gain,
        grad_qkv,
        grad_attn_out,
        grad_ffn_gain,
        grad_gate_up,
        grad_down,
    )
    global_set = (
        lax.all_gather(patch_table, "fsdp", axis=0, tiled=True),
        lax.all_gather(global_gain, "fsdp", axis=0, tiled=True),
        lax.all_gather(in_proj, "fsdp", axis=0, tiled=True),
        lax.all_gather(conv_weight, "fsdp", axis=0, tiled=True),
        lax.all_gather(conv_bias, "fsdp", axis=0, tiled=True),
        lax.all_gather(step_bias, "fsdp", axis=0, tiled=True),
        lax.all_gather(decay_log, "fsdp", axis=0, tiled=True),
        lax.all_gather(skip_gain, "fsdp", axis=0, tiled=True),
        lax.all_gather(mixer_gain, "fsdp", axis=0, tiled=True),
        lax.all_gather(out_proj, "fsdp", axis=0, tiled=True),
    )
    patch_grad_low = grad_patch_out.reshape(groups * patches, D).astype(jnp.bfloat16)
    grad_out_proj = outer_rows(mixer_low, patch_grad_low)
    grad_mixer = times_transposed(patch_grad_low, global_set[9]).reshape(groups, patches, DI)
    _, pull_mixer = jax.vjp(
        mixer_back, local_out, c_rows, cumulative, state_in, gate_z, mixer_scale
    )
    grad_local_out, grad_c_rows, grad_cumulative, grad_state_in, grad_gate_z, grad_mixer_gain = (
        pull_mixer(grad_mixer)
    )
    later_sum = entering_2((decay_total, grad_state_in), "fsdp", chain_states, identity)
    grad_summary = later_sum[1]
    grad_decay = jnp.sum(grad_summary * state_in, axis=(2, 3))
    _, pull_front = jax.vjp(mixer_front, *front_args)
    (
        grad_conv_input,
        grad_rim,
        grad_conv_weight,
        grad_conv_bias,
        grad_step_raw,
        grad_step_bias,
        grad_decay_log,
        grad_skip_gain,
    ) = pull_front((grad_local_out, grad_c_rows, grad_cumulative, grad_summary, grad_decay))
    returned = from_behind(grad_rim, "fsdp", -1)
    grad_conv_input = jnp.concatenate(
        [
            grad_conv_input[:, : patches - (KC - 1)],
            grad_conv_input[:, patches - (KC - 1) :] + returned,
        ],
        1,
    )
    grad_projected = (
        jnp.concatenate([grad_gate_z, grad_conv_input, grad_step_raw], 2)
        .reshape(groups * patches, INW)
        .astype(jnp.bfloat16)
    )
    grad_in_proj = outer_rows(global_normed, grad_projected)
    grad_normed = times_transposed(grad_projected, global_set[2]).reshape(groups, patches, D)
    _, pull_global = jax.vjp(scale_rows, patch_input, global_scale)
    grad_input_norm, grad_global_gain = pull_global(grad_normed)
    grad_input_low = (grad_input_norm + grad_patch_out).astype(jnp.bfloat16) * keep_row.astype(
        jnp.bfloat16
    )
    grad_patch_table = jnp.einsum(
        "bpjv,bpjc->jvc",
        patch_hot,
        grad_input_low.reshape(groups, patches, PATCH, DG),
        preferred_element_type=jnp.float32,
    ).reshape(PATCH * VOCAB, DG)
    owned = (
        lax.psum_scatter(
            grad_patch_table.astype(jnp.bfloat16), "fsdp", scatter_dimension=0, tiled=True
        ).astype(jnp.float32),
        lax.psum_scatter(
            grad_global_gain.astype(jnp.bfloat16), "fsdp", scatter_dimension=0, tiled=True
        ).astype(jnp.float32),
        lax.psum_scatter(
            grad_in_proj.astype(jnp.bfloat16), "fsdp", scatter_dimension=0, tiled=True
        ).astype(jnp.float32),
        lax.psum_scatter(
            grad_conv_weight.astype(jnp.bfloat16), "fsdp", scatter_dimension=0, tiled=True
        ).astype(jnp.float32),
        lax.psum_scatter(
            grad_conv_bias.astype(jnp.bfloat16), "fsdp", scatter_dimension=0, tiled=True
        ).astype(jnp.float32),
        lax.psum_scatter(
            grad_step_bias.astype(jnp.bfloat16), "fsdp", scatter_dimension=0, tiled=True
        ).astype(jnp.float32),
        lax.psum_scatter(
            grad_decay_log.astype(jnp.bfloat16), "fsdp", scatter_dimension=0, tiled=True
        ).astype(jnp.float32),
        lax.psum_scatter(
            grad_skip_gain.astype(jnp.bfloat16), "fsdp", scatter_dimension=0, tiled=True
        ).astype(jnp.float32),
        lax.psum_scatter(
            grad_mixer_gain.astype(jnp.bfloat16), "fsdp", scatter_dimension=0, tiled=True
        ).astype(jnp.float32),
        lax.psum_scatter(
            grad_out_proj.astype(jnp.bfloat16), "fsdp", scatter_dimension=0, tiled=True
        ).astype(jnp.float32),
        lax.psum_scatter(
            local_terms[0].astype(jnp.bfloat16), "fsdp", scatter_dimension=0, tiled=True
        ).astype(jnp.float32),
        lax.psum_scatter(
            local_terms[1].astype(jnp.bfloat16), "fsdp", scatter_dimension=0, tiled=True
        ).astype(jnp.float32),
        lax.psum_scatter(
            local_terms[2].astype(jnp.bfloat16), "fsdp", scatter_dimension=0, tiled=True
        ).astype(jnp.float32),
        lax.psum_scatter(
            local_terms[3].astype(jnp.bfloat16), "fsdp", scatter_dimension=0, tiled=True
        ).astype(jnp.float32),
        lax.psum_scatter(
            local_terms[4].astype(jnp.bfloat16), "fsdp", scatter_dimension=0, tiled=True
        ).astype(jnp.float32),
        lax.psum_scatter(
            local_terms[5].astype(jnp.bfloat16), "fsdp", scatter_dimension=0, tiled=True
        ).astype(jnp.float32),
        lax.psum_scatter(
            local_terms[6].astype(jnp.bfloat16), "fsdp", scatter_dimension=0, tiled=True
        ).astype(jnp.float32),
    )
    summed_all = (
        lax.psum(owned[0].astype(jnp.bfloat16), "dp").astype(jnp.float32),
        lax.psum(owned[1].astype(jnp.bfloat16), "dp").astype(jnp.float32),
        lax.psum(owned[2].astype(jnp.bfloat16), "dp").astype(jnp.float32),
        lax.psum(owned[3].astype(jnp.bfloat16), "dp").astype(jnp.float32),
        lax.psum(owned[4].astype(jnp.bfloat16), "dp").astype(jnp.float32),
        lax.psum(owned[5].astype(jnp.bfloat16), "dp").astype(jnp.float32),
        lax.psum(owned[6].astype(jnp.bfloat16), "dp").astype(jnp.float32),
        lax.psum(owned[7].astype(jnp.bfloat16), "dp").astype(jnp.float32),
        lax.psum(owned[8].astype(jnp.bfloat16), "dp").astype(jnp.float32),
        lax.psum(owned[9].astype(jnp.bfloat16), "dp").astype(jnp.float32),
        lax.psum(owned[10].astype(jnp.bfloat16), "dp").astype(jnp.float32),
        lax.psum(owned[11].astype(jnp.bfloat16), "dp").astype(jnp.float32),
        lax.psum(owned[12].astype(jnp.bfloat16), "dp").astype(jnp.float32),
        lax.psum(owned[13].astype(jnp.bfloat16), "dp").astype(jnp.float32),
        lax.psum(owned[14].astype(jnp.bfloat16), "dp").astype(jnp.float32),
        lax.psum(owned[15].astype(jnp.bfloat16), "dp").astype(jnp.float32),
        lax.psum(owned[16].astype(jnp.bfloat16), "dp").astype(jnp.float32),
    )
    return (
        activations,
        summed_all[0],
        summed_all[1],
        summed_all[2],
        summed_all[3],
        summed_all[4],
        summed_all[5],
        summed_all[6],
        summed_all[7],
        summed_all[8],
        summed_all[9],
        summed_all[10],
        summed_all[11],
        summed_all[12],
        summed_all[13],
        summed_all[14],
        summed_all[15],
        summed_all[16],
    )


def solution(mesh):
    in_specs = (
        P("dp", "fsdp"),
        P("dp", "fsdp", None),
        P("fsdp", None),
        P("fsdp"),
        P("fsdp", None),
        P("fsdp", None),
        P("fsdp"),
        P("fsdp"),
        P("fsdp"),
        P("fsdp"),
        P("fsdp"),
        P("fsdp", None),
        P("fsdp", None),
        P("fsdp"),
        P("fsdp", None),
        P("fsdp", None),
        P("fsdp"),
        P("fsdp", None),
        P("fsdp", None),
    )
    out_specs = (
        P("dp", "fsdp", None),
        P("fsdp", None),
        P("fsdp"),
        P("fsdp", None),
        P("fsdp", None),
        P("fsdp"),
        P("fsdp"),
        P("fsdp"),
        P("fsdp"),
        P("fsdp"),
        P("fsdp", None),
        P("fsdp", None),
        P("fsdp"),
        P("fsdp", None),
        P("fsdp", None),
        P("fsdp"),
        P("fsdp", None),
        P("fsdp", None),
    )
    return jax.shard_map(
        on_device, mesh=mesh, in_specs=in_specs, out_specs=out_specs, check_vma=False
    )
```

profile of v0, /device:TPU:0, one launch (start us, length us, event | category | flops | bytes accessed | tf_op | source)
XLA Modules:
  0.0 1687.3 jit_solution(6971184831470143917)
XLA Ops:
  21.5 65.4 %all-reduce.34 = (bf16[32]{0:T(256)(128)(2,1)S(1)}, bf16[32]{0:T(256)(128)(2,1)S(1)}, bf16[1024]{0:T(1024)(128)(2,1)S(1)}, bf16[2304]{0:T(1024)(128)(2,1)S(1)}, ...) all-reduce(bf16[32]{0:T(256)(128)(2,1)S(1)} %dynamic-update-slice.3, ...), channel_id=1, replica_groups=mesh['dp'=2,'fsdp'=16] {'fsdp'}, use_global_device_ids=true, to_apply=%add.21 | all-reduce | flops 5472 | bytes 21888
  86.9 17.5 %all-gather.2 = bf16[16,144,4]{1,2,0:T(4,128)(2,1)S(1)} all-gather(bf16[1,144,4]{1,2,0:T(4,128)(2,1)} %bitcast.336), channel_id=1, replica_groups=mesh['dp'=2,'fsdp'=16] {'fsdp'}, dimensions={0}, use_global_device_ids=true | all-gather | bytes 19584 | tf_op jit(solution)/shard_map/all_gather | solution.py:198
  104.7 20.8 %all_gather.76 = bf16[2048,128]{1,0:T(8,128)(2,1)S(1)} all-gather(bf16[128,128]{1,0:T(8,128)(2,1)} %param.25), channel_id=1, replica_groups=mesh['dp'=2,'fsdp'=16] {'fsdp'}, dimensions={0}, use_global_device_ids=true | all-gather | bytes 557056 | tf_op jit(solution)/shard_map/all_gather | solution.py:195
  141.9 19.9 %all-gather.3 = bf16[16,1,128]{2,1,0:T(2,128)(2,1)S(1)} all-gather(bf16[1,1,128]{2,1,0:T(2,128)(2,1)S(1)} %bitcast.337), channel_id=1, replica_groups=mesh['dp'=2,'fsdp'=16] {'fsdp'}, dimensions={0}, use_global_device_ids=true | all-gather | bytes 4352 | tf_op jit(solution)/shard_map/all_gather | solution.py:203
  162.5 20.6 %all_gather.75 = bf16[256,1024]{1,0:T(8,128)(2,1)S(1)} all-gather(bf16[16,1024]{1,0:T(8,128)(2,1)S(1)} %copy-done.54), channel_id=1, replica_groups=mesh['dp'=2,'fsdp'=16] {'fsdp'}, dimensions={0}, use_global_device_ids=true | all-gather | bytes 557056 | tf_op jit(solution)/shard_map/all_gather | solution.py:250
  184.1 19.9 %all_gather.84 = bf16[16,1,32]{2,1,0:T(2,128)(2,1)S(1)} all-gather(bf16[1,1,32]{2,1,0:T(2,128)(2,1)S(1)} %get-tuple-element.366), channel_id=1, replica_groups=mesh['dp'=2,'fsdp'=16] {'fsdp'}, dimensions={0}, use_global_device_ids=true | all-gather | bytes 1088 | tf_op jit(solution)/shard_map/all_gather | solution.py:35
  217.3 46.9 %all-gather.15.cloned.1.call-done = bf16[2048,1024]{1,0:T(8,128)(2,1)} async-done(((bf16[128,1024]{1,0:T(8,128)(2,1)}), bf16[2048,1024]{1,0:T(8,128)(2,1)}) %all-gather.15.cloned.1.call-update) | async-done | bytes 4194320 | tf_op jit(solution)/shard_map/all_gather | solution.py:204
  267.5 58.8 %all-gather.17.cloned.1.call-done = bf16[1024,3072]{1,0:T(8,128)(2,1)} async-done(((bf16[64,3072]{1,0:T(8,128)(2,1)}), bf16[1024,3072]{1,0:T(8,128)(2,1)}) %all-gather.17.cloned.1.call-update) | async-done | bytes 6291472 | tf_op jit(solution)/shard_map/all_gather | solution.py:252
  342.5 26.0 %all-gather.19.cloned.1.call-done = bf16[1024,1024]{1,0:T(8,128)(2,1)} async-done(((bf16[64,1024]{1,0:T(8,128)(2,1)}), bf16[1024,1024]{1,0:T(8,128)(2,1)}) %all-gather.19.cloned.1.call-update) | async-done | bytes 2097168 | tf_op jit(solution)/shard_map/all_gather | solution.py:253
  372.3 123.4 %all-gather.21.cloned.1.call-done = bf16[1024,8192]{1,0:T(8,128)(2,1)} async-done(((bf16[64,8192]{1,0:T(8,128)(2,1)}), bf16[1024,8192]{1,0:T(8,128)(2,1)}) %all-gather.21.cloned.1.call-update) | async-done | bytes 16777232 | tf_op jit(solution)/shard_map/all_gather | solution.py:255
  505.9 64.4 %all-gather.23.cloned.1.call-done = bf16[4096,1024]{1,0:T(8,128)(2,1)} async-done(((bf16[256,1024]{1,0:T(8,128)(2,1)}), bf16[4096,1024]{1,0:T(8,128)(2,1)}) %all-gather.23.cloned.1.call-update) | async-done | bytes 8388624 | tf_op jit(solution)/shard_map/all_gather | solution.py:256
  580.7 14.3 multiply_reduce_fusion.2
  647.7 59.6 %all-gather.27.cloned.1.call-done = bf16[512,64,128]{2,1,0:T(8,128)(2,1)} async-done(((bf16[32,64,128]{2,1,0:T(8,128)(2,1)}), bf16[512,64,128]{2,1,0:T(8,128)(2,1)}) %all-gather.27.cloned.1.call-update) | async-done | bytes 8388624 | tf_op jit(solution)/shard_map/all_gather | solution.py:55
  707.3 39.8 %while.29 = (s32[]{:T(128)}, f32[1,32,64,128]{3,2,1,0:T(8,128)S(1)}, s32[]{:T(128)}, bf16[16,1,32]{2,1,0:T(2,128)(2,1)}, bf16[16,1,32,64,128]{4,3,2,1,0:T(8,128)...) while((s32[]{:T(128)}, f32[1,32,64,128]{3,2,1,0:T(8,128)S(1)}, s32[]{:T(128)}, ...), condition=%wide.region_16.17_spmd.clone, body=%wide.region_15.16_spmd.clone.sunk | while | flops 1310760 | bytes 2621935 | solution.py:73
  820.4 59.9 %all-reduce.33 = (bf16[1024]{0:T(1024)(128)(2,1)S(1)}, bf16[2304]{0:T(1024)(128)(2,1)S(1)}, bf16[32]{0:T(256)(128)(2,1)S(1)}, bf16[32]{0:T(256)(128)(2,1)S(1)}, ...) all-reduce(bf16[1024]{0:T(1024)(128)(2,1)S(1)} %get-tuple-element.2, ...), channel_id=5, replica_groups=mesh['dp'=2,'fsdp'=16] {'fsdp'}, use_global_device_ids=true, to_apply=%region_28.29.clone | all-reduce | flops 7520 | bytes 30080
  886.4 45.8 %reduce-scatter.12.cloned.1.call-done = bf16[128,128]{1,0:T(8,128)(2,1)} async-done(((bf16[2048,128]{1,0:T(8,128)(2,1)}), bf16[128,128]{1,0:T(8,128)(2,1)}) %reduce-scatter.12.cloned.1.call-update) | async-done | bytes 32784 | tf_op jit(solution)/shard_map/reduce_scatter | solution.py:378
  932.3 64.4 %reduce-scatter.22.cloned.1.call-done = bf16[64,1024]{1,0:T(8,128)(2,1)} async-done(((bf16[1024,1024]{1,0:T(8,128)(2,1)}), bf16[64,1024]{1,0:T(8,128)(2,1)}) %reduce-scatter.22.cloned.1.call-update) | async-done | bytes 131088 | tf_op jit(solution)/shard_map/reduce_scatter | solution.py:417
  996.7 75.6 %reduce-scatter.16.cloned.1.call-done = bf16[128,1024]{1,0:T(8,128)(2,1)} async-done(((bf16[2048,1024]{1,0:T(8,128)(2,1)}), bf16[128,1024]{1,0:T(8,128)(2,1)}) %reduce-scatter.16.cloned.1.call-update) | async-done | bytes 262160 | tf_op jit(solution)/shard_map/reduce_scatter | solution.py:405
  1072.3 88.0 %reduce-scatter.20.cloned.1.call-done = bf16[64,3072]{1,0:T(8,128)(2,1)} async-done(((bf16[1024,3072]{1,0:T(8,128)(2,1)}), bf16[64,3072]{1,0:T(8,128)(2,1)}) %reduce-scatter.20.cloned.1.call-update) | async-done | bytes 393232 | tf_op jit(solution)/shard_map/reduce_scatter | solution.py:414
  1160.3 106.5 %reduce-scatter.26.cloned.1.call-done = bf16[256,1024]{1,0:T(8,128)(2,1)} async-done(((bf16[4096,1024]{1,0:T(8,128)(2,1)}), bf16[256,1024]{1,0:T(8,128)(2,1)}) %reduce-scatter.26.cloned.1.call-update) | async-done | bytes 524304 | tf_op jit(solution)/shard_map/reduce_scatter | solution.py:426
  1266.7 181.0 %reduce-scatter.24.cloned.1.call-done = bf16[64,8192]{1,0:T(8,128)(2,1)} async-done(((bf16[1024,8192]{1,0:T(8,128)(2,1)}), bf16[64,8192]{1,0:T(8,128)(2,1)}) %reduce-scatter.24.cloned.1.call-update) | async-done | bytes 1048592 | tf_op jit(solution)/shard_map/reduce_scatter | solution.py:423
  1447.7 112.6 %reduce-scatter.14.cloned.1.call-done = bf16[64,4384]{1,0:T(8,128)(2,1)} async-done(((bf16[1024,4384]{1,0:T(8,128)(2,1)}), bf16[64,4384]{1,0:T(8,128)(2,1)}) %reduce-scatter.14.cloned.1.call-update) | async-done | bytes 561168 | tf_op jit(solution)/shard_map/reduce_scatter | solution.py:384
  1565.6 19.9 %all-reduce.40.cloned.1.call-done = (bf16[128,128]{1,0:T(8,128)(2,1)}, bf16[64]{0:T(256)(128)(2,1)}, bf16[144,4]{0,1:T(4,128)(2,1)}, bf16[144]{0:T(256)(128)(2,1...) async-done(((bf16[128,128]{1,0:T(8,128)(2,1)}, ...) | async-done | bytes 67644 | tf_op jit(solution)/shard_map/psum | solution.py:431
  1598.9 71.5 %all-reduce.42.cloned.1.call-done = (bf16[64,4384]{1,0:T(8,128)(2,1)}, bf16[128,1024]{1,0:T(8,128)(2,1)}, bf16[64,3072]{1,0:T(8,128)(2,1)}, bf16[64,1024]{1,0:T(...) async-done(((bf16[64,4384]{1,0:T(8,128)(2,1)}, bf16[128,1024]{1,0:T(8,128)(2,1)}, bf16[64,3072]{1,0:T(8,128)(2,1)}, bf16[64,1024]{1,0:T(8,128)(2,1)}, ...) | async-done | bytes 2920464 | tf_op jit(solution)/shard_map/psum | solution.py:433
  (445 shorter events, 283.9 us)
Async XLA Ops:
  7.2 118.8 %all-gather.13.cloned.1.call-start = ((), (), s32[]{:S(2)}) async-start(), calls=%async_computation.9 | async-start | bytes 9748480 | tf_op jit(solution)/shard_map/all_gather | solution.py:197
  7.9 205.0 %all-gather.25.cloned.1.call-start = ((), (), s32[]{:S(2)}) async-start(), calls=%async_computation.23 | async-start | bytes 8912896 | tf_op jit(solution)/shard_map/all_gather | solution.py:35
  19.1 106.4 %collective-permute-start = (s32[1,8]{1,0:T(1,128)S(1)}, s32[1,8]{1,0:T(1,128)S(1)}, u32[]{:S(2)}, u32[]{:S(2)}) collective-permute-start(s32[1,8]{1,0:T(1,128)S(1)} %slice_bitcast_fusion), channel_id=1, source_target_pairs={{0,1},{1,2},{2,3},{3,4},{4,5},{5,6},{6,7},{7,8},{8,9},{9,10},{10,1... | collective-permute-start | bytes 104 | tf_op jit(solution)/shard_map/ppermute | solution.py:29
  131.2 3.1 collective-permute-start.1
  138.0 126.2 %all-gather.15.cloned.1.call-start = ((), (), s32[]{:S(2)}) async-start(), calls=%async_computation.10 | async-start | bytes 4456448 | tf_op jit(solution)/shard_map/all_gather | solution.py:204
  138.8 187.5 %all-gather.17.cloned.1.call-start = ((), (), s32[]{:S(2)}) async-start(), calls=%async_computation.11 | async-start | bytes 6684672 | tf_op jit(solution)/shard_map/all_gather | solution.py:252
  139.3 229.1 %all-gather.19.cloned.1.call-start = ((), (), s32[]{:S(2)}) async-start(), calls=%async_computation.12 | async-start | bytes 2228224 | tf_op jit(solution)/shard_map/all_gather | solution.py:253
  139.9 355.8 %all-gather.21.cloned.1.call-start = ((), (), s32[]{:S(2)}) async-start(), calls=%async_computation.13 | async-start | bytes 17825792 | tf_op jit(solution)/shard_map/all_gather | solution.py:255
  140.5 429.8 %all-gather.23.cloned.1.call-start = ((), (), s32[]{:S(2)}) async-start(), calls=%async_computation.14 | async-start | bytes 8912896 | tf_op jit(solution)/shard_map/all_gather | solution.py:256
  141.3 566.1 %all-gather.27.cloned.1.call-start = ((), (), s32[]{:S(2)}) async-start(), calls=%async_computation.24 | async-start | bytes 8912896 | tf_op jit(solution)/shard_map/all_gather | solution.py:55
  267.5 351.9 %copy-start.64 = (f32[128]{0:T(128)}, f32[128]{0:T(128)S(1)}, u32[]{:S(2)}) copy-start(f32[128]{0:T(128)S(1)} %fusion.128) | copy-start | bytes 1540
  370.7 224.3 %copy-start.60 = (f32[128]{0:T(128)}, f32[128]{0:T(128)S(1)}, u32[]{:S(2)}) copy-start(f32[128]{0:T(128)S(1)} %fusion.129) | copy-start | bytes 1540
  634.3 250.7 %reduce-scatter.28.cloned.1.call-start = ((), (), s32[]{:S(2)}) async-start(), calls=%async_computation.25 | async-start | bytes 626688
  761.9 124.5 %reduce-scatter.18.cloned.1.call-start = ((), (), s32[]{:S(2)}) async-start(), calls=%async_computation.18 | async-start | bytes 557056 | tf_op jit(solution)/shard_map/reduce_scatter | solution.py:408
  766.7 165.5 %reduce-scatter.12.cloned.1.call-start = ((), (), s32[]{:S(2)}) async-start(), calls=%async_computation.15 | async-start | bytes 557056 | tf_op jit(solution)/shard_map/reduce_scatter | solution.py:378
  772.3 3.1 collective-permute-start.2
  783.3 213.4 %reduce-scatter.22.cloned.1.call-start = ((), (), s32[]{:S(2)}) async-start(), calls=%async_computation.20 | async-start | bytes 2228224 | tf_op jit(solution)/shard_map/reduce_scatter | solution.py:417
  785.5 286.8 %reduce-scatter.16.cloned.1.call-start = ((), (), s32[]{:S(2)}) async-start(), calls=%async_computation.17 | async-start | bytes 4456448 | tf_op jit(solution)/shard_map/reduce_scatter | solution.py:405
  788.9 371.4 %reduce-scatter.20.cloned.1.call-start = ((), (), s32[]{:S(2)}) async-start(), calls=%async_computation.19 | async-start | bytes 6684672 | tf_op jit(solution)/shard_map/reduce_scatter | solution.py:414
  793.5 473.2 %reduce-scatter.26.cloned.1.call-start = ((), (), s32[]{:S(2)}) async-start(), calls=%async_computation.22 | async-start | bytes 8912896 | tf_op jit(solution)/shard_map/reduce_scatter | solution.py:426
  800.5 647.2 %reduce-scatter.24.cloned.1.call-start = ((), (), s32[]{:S(2)}) async-start(), calls=%async_computation.21 | async-start | bytes 17825792 | tf_op jit(solution)/shard_map/reduce_scatter | solution.py:423
  811.6 748.7 %reduce-scatter.14.cloned.1.call-start = ((), (), s32[]{:S(2)}) async-start(), calls=%async_computation.16 | async-start | bytes 9748480 | tf_op jit(solution)/shard_map/reduce_scatter | solution.py:384
  817.5 768.0 %all-reduce.40.cloned.1.call-start = ((), (), s32[]{:S(2)}) async-start(), calls=%async_computation.26 | async-start | bytes 143360 | tf_op jit(solution)/shard_map/psum | solution.py:431
  932.2 738.1 %all-reduce.42.cloned.1.call-start = ((), (), s32[]{:S(2)}) async-start(), calls=%async_computation.27 | async-start | bytes 5865472 | tf_op jit(solution)/shard_map/psum | solution.py:433
  (89 other events, 2067.0 us)
Sparse Core Ops, SparseCore 0:
  10.3 83.0 all-gather.12
  138.2 74.6 all-gather.24
  215.0 49.1 all-gather.14
  266.3 59.9 all-gather.16
  328.3 40.1 all-gather.18
  370.5 125.1 all-gather.20
  497.8 72.4 all-gather.22
  634.4 72.8 all-gather.26
  762.0 52.6 reduce-scatter.27
  818.1 55.1 reduce-scatter.17
  876.9 55.2 reduce-scatter.11
  935.8 60.8 reduce-scatter.21
  1000.6 71.6 reduce-scatter.15
  1076.1 84.1 reduce-scatter.19
  1164.2 102.5 reduce-scatter.25
  1270.7 176.9 reduce-scatter.23
  1451.7 108.5 reduce-scatter.13
  1564.2 21.2 all-reduce.39
  1588.2 82.1 all-reduce.41
where the time goes:
time: 1700 us; the launch traced here: 1690 us
  waiting for transfers between devices  1160 us (68%)
  blocking collectives  224 us (13%)
  matrix products  148 us (9%)
  other arithmetic  82.8 us (5%)
  local copies, waits for them, and re-layouts  46 us (3%)
  between operations  20.2 us (1%)
    reduce_scatter x1, waiting for transfers between devices, on_device(): lax.psum_scatter(local_terms[5].astype(jnp.bfloat16), 'fsdp', scatter_dim...  181 us
    unnamed x2, blocking collectives  125 us
    all_gather x1, waiting for transfers between devices, on_device(): lax.all_gather(gate_up, 'fsdp', axis=0, tiled=True)  123 us
    reduce_scatter x1, waiting for transfers between devices, on_device(): lax.psum_scatter(grad_in_proj.astype(jnp.bfloat16), 'fsdp', scatter_dimen...  113 us
    reduce_scatter x1, waiting for transfers between devices, on_device(): lax.psum_scatter(local_terms[6].astype(jnp.bfloat16), 'fsdp', scatter_dim...  106 us
    reduce_scatter x1, waiting for transfers between devices, on_device(): lax.psum_scatter(local_terms[2].astype(jnp.bfloat16), 'fsdp', scatter_dim...  88 us
    reduce_scatter x1, waiting for transfers between devices, on_device(): lax.psum_scatter(grad_out_proj.astype(jnp.bfloat16), 'fsdp', scatter_dime...  75.6 us
    psum x1, waiting for transfers between devices, on_device(): lax.psum(owned[2].astype(jnp.bfloat16), 'dp').astype(jnp.float32)  71.5 us
  transfers between devices with their start and end apart: 22, of which 18 were waited for; matrix products, arithmetic and copies ran while one was open for 8% of the time, Pallas kernels for 0%

commit v1 on v0

v1 whole, which is shorter than its diff:
```python
import functools

import jax
import jax.numpy as jnp
from jax import lax
from jax.experimental import pallas as pl
from jax.experimental.pallas import tpu as pltpu
from jax.sharding import PartitionSpec as P

D = 1024
NST = 128
HM = 32
HA = 16
FF = 4096
VOCAB = 256
KC = 4
PATCH = 8
DI = 2048
PM = 64
DA = 64
DG = 128
XBC = 2304
BC = XBC - DI
EPS = 1e-05
PAIRS = HA // 2
highest = lax.Precision.HIGHEST
bf16 = jnp.bfloat16
f32 = jnp.float32
VM = pl.BlockSpec(memory_space=pltpu.VMEM)


def grid_of(n):
    outer = max(n // 8, 1) if n >= 8 else 1
    return n // (2 * outer), outer


class Place:
    def __init__(self, n):
        self.n = n
        self.A, self.B = grid_of(n)
        me = lax.axis_index("fsdp")
        self.me = me
        self.c = me % 2
        self.b = (me // 2) % self.B
        self.a = me // (2 * self.B)

    def at(self, a, b, c):
        return (a * self.B + b) * 2 + c


def remote(src, dst, send, recv, peer):
    return pltpu.make_async_remote_copy(
        src_ref=src,
        dst_ref=dst,
        send_sem=send,
        recv_sem=recv,
        device_id={"fsdp": peer},
        device_id_type=pl.DeviceIdType.MESH,
    )


def gather_steps(pc, src, out, sems):
    send, recv = sems
    A, B = pc.A, pc.B
    started = []
    slot = [0]

    def push(block, where, peer):
        cp = remote(block, out.at[where], send.at[slot[0]], recv.at[where], peer)
        slot[0] += 1
        cp.start()
        started.append(cp)

    def arrived(where):
        remote(src, out.at[where], send.at[0], recv.at[where], pc.me).wait_recv()

    for off in range(1, A):
        push(src, pc.me, pc.at((pc.a + off) % A, pc.b, pc.c))
    for k in range(1, B):
        push(src, pc.me, pc.at(pc.a, (pc.b + k) % B, pc.c))
    push(src, pc.me, pc.at(pc.a, pc.b, 1 - pc.c))
    out[pc.me] = src[...]
    yield
    for off in range(1, A):
        where = pc.at((pc.a - off + A) % A, pc.b, pc.c)
        arrived(where)
        for k in range(1, B):
            push(out.at[where], where, pc.at(pc.a, (pc.b + k) % B, pc.c))
        push(out.at[where], where, pc.at(pc.a, pc.b, 1 - pc.c))
    yield
    for off in range(A):
        for k in range(1, B):
            where = pc.at((pc.a - off + A) % A, (pc.b - k + B) % B, pc.c)
            arrived(where)
            push(out.at[where], where, pc.at(pc.a, pc.b, 1 - pc.c))
    yield
    for a in range(A):
        for b in range(B):
            arrived(pc.at(a, b, 1 - pc.c))
    for cp in started:
        cp.wait_send()


def exchange_steps(pc, src, out, sems):
    send, recv = sems
    n = pc.n
    started = []
    for k in range(1, n):
        peer = (pc.me + k) % n
        cp = remote(src.at[peer], out.at[pc.me], send.at[k - 1], recv.at[pc.me], peer)
        cp.start()
        started.append(cp)
    out[pc.me] = src[pc.me]
    yield
    yield
    yield
    for k in range(1, n):
        peer = (pc.me + k) % n
        remote(src.at[peer], out.at[peer], send.at[k - 1], recv.at[peer], pc.me).wait_recv()
    for cp in started:
        cp.wait_send()


def sum_steps(pc, src, out, scratch):
    r1, s1, r2, s2, r3, send1, recv1, send2, recv2, send3, recv3 = scratch
    A, B = pc.A, pc.B
    started = []
    order = [(pc.a + off) % A for off in list(range(1, A)) + [0]]

    def begin(cp):
        cp.start()
        started.append(cp)

    def copy1(a):
        return remote(
            src.at[a, :, 1 - pc.c], r1.at[a], send1.at[a], recv1.at[a], pc.at(pc.a, pc.b, 1 - pc.c)
        )

    def copy2(a, k):
        to = (pc.b + k) % B
        return remote(
            s1.at[a, to], r2.at[a, k - 1], send2.at[a, k - 1], recv2.at[a, k - 1],
            pc.at(pc.a, to, pc.c),
        )

    def copy3(a, off):
        return remote(
            s2.at[a], r3.at[off - 1], send3.at[off - 1], recv3.at[off - 1], pc.at(a, pc.b, pc.c)
        )

    for a in order:
        begin(copy1(a))
    yield
    for a in order:
        copy1(a).wait_recv()
        for k in range(1, B):
            to = (pc.b + k) % B
            s1[a, to] = (src[a, to, pc.c].astype(f32) + r1[a, to].astype(f32)).astype(s1.dtype)
            begin(copy2(a, k))
    yield
    for off, a in zip(list(range(1, A)) + [0], order):
        total = src[a, pc.b, pc.c].astype(f32) + r1[a, pc.b].astype(f32)
        for k in range(1, B):
            copy2(a, k).wait_recv()
            total = total + r2[a, k - 1].astype(f32)
        if off > 0:
            s2[a] = total.astype(s2.dtype)
            begin(copy3(a, off))
        else:
            out[...] = total
    yield
    for off in range(1, A):
        copy3(pc.a, off).wait_recv()
        out[...] += r3[off - 1].astype(f32)
    for cp in started:
        cp.wait_send()


def scratch_of(kind, x, n):
    A, B = grid_of(n)
    dma = pltpu.SemaphoreType.DMA
    if kind == "gather":
        return [dma((2 * n,)), dma((n,))]
    if kind == "exchange":
        return [dma((n,)), dma((n,))]
    r, c = x.shape[-2:]
    return [
        pltpu.VMEM((A, B, r, c), x.dtype),
        pltpu.VMEM((A, B, r, c), x.dtype),
        pltpu.VMEM((A, max(B - 1, 1), r, c), x.dtype),
        pltpu.VMEM((A, r, c), x.dtype),
        pltpu.VMEM((max(A - 1, 1), r, c), x.dtype),
        dma((A,)),
        dma((A,)),
        dma((A, max(B - 1, 1))),
        dma((A, max(B - 1, 1))),
        dma((max(A - 1, 1),)),
        dma((max(A - 1, 1),)),
    ]


STEPS = {"gather": gather_steps, "exchange": exchange_steps, "sum": sum_steps}


def comm_kernel(kinds, counts, n, *refs):
    m = len(kinds)
    ins, outs, rest = refs[:m], refs[m : 2 * m], refs[2 * m :]
    pc = Place(n)
    barrier = pltpu.get_barrier_semaphore()
    if "exchange" in kinds:
        peers = [(pc.me + k) % n for k in range(1, n)]
    else:
        peers = [pc.at((pc.a + k) % pc.A, pc.b, pc.c) for k in range(1, pc.A)]
        peers += [pc.at(pc.a, (pc.b + k) % pc.B, pc.c) for k in range(1, pc.B)]
        peers += [pc.at(pc.a, pc.b, 1 - pc.c)]
    for peer in peers:
        pl.semaphore_signal(
            barrier, inc=1, device_id={"fsdp": peer}, device_id_type=pl.DeviceIdType.MESH
        )
    pl.semaphore_wait(barrier, len(peers))
    live = []
    for kind, count, src, out in zip(kinds, counts, ins, outs):
        live.append(STEPS[kind](pc, src, out, rest[:count]))
        rest = rest[count:]
    while live:
        left = []
        for steps in live:
            try:
                next(steps)
                left.append(steps)
            except StopIteration:
                pass
        live = left


def communicate(n, cid, *jobs):
    A, B = grid_of(n)
    kinds, ins, outs, scratch, counts = [], [], [], [], []
    for kind, x in jobs:
        kinds.append(kind)
        if kind == "gather":
            outs.append(jax.ShapeDtypeStruct((n,) + x.shape, x.dtype))
        elif kind == "exchange":
            outs.append(jax.ShapeDtypeStruct(x.shape, x.dtype))
        else:
            outs.append(jax.ShapeDtypeStruct(x.shape[-2:], f32))
        own = scratch_of(kind, x, n)
        counts.append(len(own))
        scratch += own
        ins.append(x.reshape((A, B, 2) + x.shape[1:]) if kind == "sum" else x)
    return pl.pallas_call(
        functools.partial(comm_kernel, tuple(kinds), tuple(counts), n),
        out_shape=tuple(outs),
        in_specs=[VM] * len(ins),
        out_specs=tuple([VM] * len(ins)),
        scratch_shapes=scratch,
        compiler_params=pltpu.CompilerParams(
            collective_id=cid, has_side_effects=True, vmem_limit_bytes=60 * 1024 * 1024
        ),
        name="comm_%d" % cid,
    )(*ins)


def rms_back(dy, v, gain, r):
    dyg = dy * gain
    m = jnp.mean(dyg * v, axis=-1, keepdims=True)
    return r * dyg - v * (r * r * r) * m, jnp.sum(dy * v * r, axis=0)


def row_scale(v):
    return lax.rsqrt(jnp.mean(v * v, axis=-1, keepdims=True) + EPS)


def dot(a, b, dims=((1,), (0,))):
    return lax.dot_general(a, b, (dims, ((), ())), preferred_element_type=f32)


NT = ((1,), (1,))
TN = ((0,), (0,))


def head_parts(rows):
    lane = lax.broadcasted_iota(jnp.int32, (rows, 2 * DA), 1)
    ri = lax.broadcasted_iota(jnp.int32, (rows, rows), 0)
    ci = lax.broadcasted_iota(jnp.int32, (rows, rows), 1)
    allowed = jnp.logical_and(ri // PATCH == ci // PATCH, ci <= ri)
    return (lane < DA, lane >= DA), allowed


def weights_of(q, k, allowed):
    s = dot(q, k, NT) * (DA**-0.5)
    s = jnp.where(allowed, s, -1e30)
    e = jnp.exp(s - jnp.max(s, axis=-1, keepdims=True))
    return e / jnp.sum(e, axis=-1, keepdims=True)


def attend_kernel(qkv_ref, out_ref):
    rows = qkv_ref.shape[0]
    sides, allowed = head_parts(rows)
    for pair in range(PAIRS):
        lo = pair * 2 * DA
        q = qkv_ref[:, lo : lo + 2 * DA].astype(bf16)
        k = qkv_ref[:, D + lo : D + lo + 2 * DA].astype(bf16)
        v = qkv_ref[:, 2 * D + lo : 2 * D + lo + 2 * DA].astype(bf16)
        parts = []
        for side in sides:
            p = weights_of(jnp.where(side, q, jnp.zeros_like(q)), k, allowed)
            parts.append(dot(p.astype(bf16), v))
        out_ref[:, lo : lo + 2 * DA] = jnp.where(sides[0], parts[0], parts[1]).astype(bf16)


def attend(qkv):
    return pl.pallas_call(
        attend_kernel,
        out_shape=jax.ShapeDtypeStruct((qkv.shape[0], D), bf16),
        in_specs=[VM],
        out_specs=VM,
        name="attend",
    )(qkv)


def attend_back_kernel(qkv_ref, g_ref, out_ref):
    rows = qkv_ref.shape[0]
    sides, allowed = head_parts(rows)
    scale = DA**-0.5
    for pair in range(PAIRS):
        lo = pair * 2 * DA
        q = qkv_ref[:, lo : lo + 2 * DA].astype(bf16)
        k = qkv_ref[:, D + lo : D + lo + 2 * DA].astype(bf16)
        v = qkv_ref[:, 2 * D + lo : 2 * D + lo + 2 * DA].astype(bf16)
        g = g_ref[:, lo : lo + 2 * DA].astype(bf16)
        dq, dk, dv = [], [], []
        for side in sides:
            p = weights_of(jnp.where(side, q, jnp.zeros_like(q)), k, allowed)
            dp = dot(jnp.where(side, g, jnp.zeros_like(g)), v, NT)
            ds = p * (dp - jnp.sum(dp * p, axis=-1, keepdims=True))
            ds = ds.astype(bf16)
            dq.append(dot(ds, k) * scale)
            dk.append(dot(ds, q, TN) * scale)
            dv.append(dot(p.astype(bf16), g, TN))
        for j, parts in enumerate((dq, dk, dv)):
            out_ref[:, j * D + lo : j * D + lo + 2 * DA] = jnp.where(
                sides[0], parts[0], parts[1]
            ).astype(bf16)


def attend_back(qkv, g):
    return pl.pallas_call(
        attend_back_kernel,
        out_shape=jax.ShapeDtypeStruct(qkv.shape, bf16),
        in_specs=[VM, VM],
        out_specs=VM,
        name="attend_back",
    )(qkv, g)


def mixer(conv_in, taps, bias, step_raw, step_bias, decay_log, skip, gate, width):
    length = conv_in.shape[0]
    heads = width // PM
    padded = jnp.concatenate([jnp.zeros((KC - 1, conv_in.shape[1]), f32), conv_in], 0)
    summed = bias
    for k in range(KC):
        summed = summed + padded[k : k + length] * taps[k]
    out = jax.nn.silu(summed)
    x, b, c = out[:, :width], out[:, width : width + NST], out[:, width + NST :]
    step = jax.nn.softplus(step_raw + step_bias)
    ri = lax.broadcasted_iota(jnp.int32, (length, length), 0)
    ci = lax.broadcasted_iota(jnp.int32, (length, length), 1)
    causal = ci <= ri
    logs = step * -jnp.exp(decay_log)
    total = jnp.dot(causal.astype(f32), logs, precision=highest).T
    spread = total[:, :, None] - total[:, None, :]
    decay = jnp.exp(jnp.where(causal[None], spread, -jnp.inf))
    cb = lax.dot_general(c, b, (NT, ((), ())), precision=highest)
    xh = x.reshape(length, heads, PM)
    scaled = xh * step[..., None]
    joined = jnp.einsum("htu,uhp->thp", cb[None] * decay, scaled, precision=highest)
    joined = joined + skip[:, None] * xh
    return joined.reshape(length, width) * jax.nn.silu(gate)


def across(x, dp):
    if dp == 1:
        return x.astype(f32)
    if dp > 2:
        return lax.psum(x, "dp").astype(f32)
    x = lax.optimization_barrier(x)
    return x.astype(f32) + lax.ppermute(x, "dp", [(0, 1), (1, 0)]).astype(f32)


def on_device(
    n,
    dp,
    byte_ids,
    cotangent,
    patch_table,
    global_gain,
    in_proj,
    conv_weight,
    conv_bias,
    step_bias,
    decay_log,
    skip_gain,
    mixer_gain,
    out_proj,
    byte_table,
    local_gain,
    qkv_proj,
    attn_out,
    ffn_gain,
    gate_up,
    down_proj,
):
    me = lax.axis_index("fsdp")
    _, L = byte_ids.shape
    own_p = L // PATCH
    T = own_p * n
    R = L * n
    dn, fn, wn, hn = D // n, FF // n, DI // n, HM // n
    xn = XBC // n
    ids = byte_ids.reshape(L)

    gather = functools.partial(lax.all_gather, axis_name="fsdp", axis=0, tiled=True)
    qkv_full = gather(qkv_proj)
    byte_full = gather(byte_table)
    attn_full = gather(attn_out)
    cot_all = gather(cotangent.reshape(L, D))

    zx = in_proj[:, : 2 * DI].reshape(dn, 2, n, wn).transpose(2, 0, 1, 3).reshape(n, dn, 2 * wn)
    shared = jnp.pad(in_proj[:, 2 * DI :], ((0, 0), (0, 384 - (BC + HM))))
    gu = gate_up.reshape(dn, 2, n, fn).transpose(2, 0, 1, 3).reshape(n, dn, 2 * fn)
    vectors = [global_gain, local_gain, ffn_gain, conv_weight.reshape(-1), conv_bias,
               step_bias, decay_log, skip_gain]
    sizes = [v.shape[0] for v in vectors]
    packed = jnp.concatenate(vectors)
    packed = jnp.pad(packed, (0, 2048 - packed.shape[0])).reshape(16, 128)
    ids_all, small, table, shared_w, zx_w, gu_w = communicate(
        n, 0,
        ("gather", ids.reshape(1, L)),
        ("gather", packed),
        ("gather", patch_table),
        ("gather", shared),
        ("exchange", zx),
        ("exchange", gu),
    )
    small = small.reshape(n, 2048).astype(f32)
    full = []
    at = 0
    for s in sizes:
        full.append(small[:, at : at + s].reshape(-1))
        at += s
    g_gain, l_gain, f_gain, taps_all, bias_all = full[:5]
    taps_all = taps_all.reshape(XBC, KC)
    taps = jnp.concatenate(
        [lax.dynamic_slice_in_dim(taps_all, me * wn, wn, 0), taps_all[DI:]], 0
    ).T
    bias = jnp.concatenate([lax.dynamic_slice_in_dim(bias_all, me * wn, wn, 0), bias_all[DI:]], 0)
    w_mix = jnp.concatenate([zx_w.reshape(D, 2 * wn), shared_w.reshape(D, 384)], 1)
    w_gu = gu_w.reshape(D, 2 * fn)
    table = table.reshape(PATCH, VOCAB, DG)

    grid = ids_all.reshape(T, PATCH)
    earlier = jnp.concatenate([jnp.full((1, PATCH), -1, jnp.int32), grid[:-1]], 0)
    hot = (earlier[..., None] == jnp.arange(VOCAB, dtype=jnp.int32)).astype(bf16)
    patch_input = jnp.einsum("pjv,jvc->pjc", hot, table, preferred_element_type=f32).reshape(T, D)
    r_g = row_scale(patch_input)
    normed = (patch_input * r_g * g_gain).astype(bf16)
    proj = dot(normed, w_mix)
    gate_z = proj[:, :wn]
    conv_in = proj[:, wn : 2 * wn + BC]
    dt_all = proj[:, 2 * wn + BC : 2 * wn + BC + HM]
    dt_raw = lax.dynamic_slice_in_dim(dt_all, me * hn, hn, 1)
    y, pull_mixer = jax.vjp(
        functools.partial(mixer, width=wn),
        conv_in, taps, bias, dt_raw, step_bias.astype(f32), decay_log.astype(f32),
        skip_gain.astype(f32), gate_z,
    )
    m_gain = mixer_gain.astype(f32)
    part = dot((y * m_gain).astype(bf16), out_proj)
    squares = jnp.broadcast_to(jnp.sum(y * y, axis=-1, keepdims=True), (T, 128))
    payload = jnp.concatenate([part, squares], 1).astype(bf16).reshape(n, own_p, D + 128)
    (summed,) = communicate(n, 1, ("sum", payload))
    out_sum = summed[:, :D]
    r_m = lax.rsqrt(summed[:, D : D + 1] * (1.0 / DI) + EPS)
    own_input = lax.dynamic_slice_in_dim(patch_input, me * own_p, own_p, 0)
    own_r_g = lax.dynamic_slice_in_dim(r_g, me * own_p, own_p, 0)
    patch_out = own_input + r_m * out_sum

    byte_hot = (ids[:, None] == jnp.arange(VOCAB, dtype=jnp.int32)[None, :]).astype(bf16)
    spread = jnp.broadcast_to(patch_out[:, None, :], (own_p, PATCH, D)).reshape(L, D)
    stream = dot(byte_hot, byte_full) + spread
    r_l = row_scale(stream)
    first_norm = (stream * r_l * l_gain).astype(bf16)
    qkv = dot(first_norm, qkv_full)
    attended = attend(qkv)
    residual = stream + dot(attended, attn_full)
    r_f = row_scale(residual)
    second_norm = (residual * r_f * f_gain).astype(bf16)

    (x_all,) = communicate(n, 2, ("gather", second_norm))
    x_all = x_all.reshape(R, D)
    gates = dot(x_all, w_gu)
    gate, up = gates[:, :fn], gates[:, fn:]
    sig = jax.nn.sigmoid(gate)
    act = gate * sig
    hidden = (act * up).astype(bf16)
    y_part = dot(hidden, down_proj)
    g_hidden = dot(cot_all, down_proj, NT)
    d_gate = g_hidden * up * (sig * (1.0 + gate * (1.0 - sig)))
    grad_gates = jnp.concatenate([d_gate, g_hidden * act], 1).astype(bf16)
    gs_part = dot(grad_gates, w_gu, NT)
    both = jnp.concatenate([y_part, gs_part], 1).astype(bf16).reshape(n, L, 2 * D)
    (both,) = communicate(n, 3, ("sum", both))
    activations = (residual + both[:, :D]).astype(bf16).reshape(1, L, D)
    grad_second = both[:, D:]
    grad_down = dot(hidden, cot_all, TN).astype(bf16)
    grad_gu = dot(x_all, grad_gates, TN).astype(bf16).reshape(n, dn, 2 * fn)
    down_out = across(grad_down, dp)

    res_norm, d_f_gain = rms_back(grad_second, residual, f_gain, r_f)
    grad_residual = cotangent.reshape(L, D).astype(f32) + res_norm
    res_low = grad_residual.astype(bf16)
    scatter = functools.partial(
        lax.psum_scatter, axis_name="fsdp", scatter_dimension=0, tiled=True
    )
    attn_g = scatter(dot(attended, res_low, TN).astype(bf16))
    g_att = dot(res_low, attn_full, NT)
    grad_qkv_rows = attend_back(qkv, g_att)
    qkv_g = scatter(dot(first_norm, grad_qkv_rows, TN).astype(bf16))
    grad_first = dot(grad_qkv_rows, qkv_full, NT)
    stream_norm, d_l_gain = rms_back(grad_first, stream, l_gain, r_l)
    grad_stream = grad_residual + stream_norm
    byte_g = scatter(dot(byte_hot, grad_stream.astype(bf16), TN).astype(bf16))
    gpo_own = grad_stream.reshape(own_p, PATCH, D).sum(axis=1)
    gpo_low = gpo_own.astype(bf16)
    mean_own = jnp.sum(gpo_low.astype(f32) * out_sum, axis=-1, keepdims=True) * (1.0 / DI)
    lane = lax.broadcasted_iota(jnp.int32, (own_p, 128), 1)
    scal = jnp.where(lane == 0, r_m, mean_own)
    gpo, scal, gu_back = communicate(
        n, 4, ("gather", gpo_low), ("gather", scal), ("exchange", grad_gu)
    )
    gpo = gpo.reshape(T, D)
    scal = scal.reshape(T, 128)
    r_m_all, mean_all = scal[:, 0:1], scal[:, 1:2]
    gu_rows = gu_back.reshape(n, dn, 2, fn).transpose(1, 2, 0, 3).reshape(dn, 2 * FF)
    gu_out = across(gu_rows, dp)

    mixer_low = (y * r_m_all * m_gain).astype(bf16)
    op_out = across(dot(mixer_low, gpo, TN).astype(bf16), dp)
    g_mix = dot(gpo, out_proj, NT)
    d_m_gain = jnp.sum(g_mix * y * r_m_all, axis=0)
    grad_y = r_m_all * (g_mix * m_gain) - y * (r_m_all * r_m_all * r_m_all) * mean_all
    d_conv, d_taps, d_bias, d_dt, d_step_b, d_decay, d_skip, d_z = pull_mixer(grad_y)
    dt_cols = lax.dynamic_update_slice(jnp.zeros((T, 384 - BC), f32), d_dt, (0, me * hn))
    gp = jnp.concatenate([d_z, d_conv, dt_cols], 1).astype(bf16)
    gn_part = dot(gp, w_mix, NT).astype(bf16).reshape(n, own_p, D)
    g_w = dot(normed, gp, TN).astype(bf16).reshape(n, dn, 2 * wn + 384)
    zx_g, sh_g, gn = communicate(
        n, 5, ("exchange", g_w[:, :, : 2 * wn]), ("sum", g_w[:, :, 2 * wn :]), ("sum", gn_part)
    )
    zx_rows = zx_g.reshape(n, dn, 2, wn).transpose(1, 2, 0, 3).reshape(dn, 2 * DI)
    in_rows = jnp.concatenate([zx_rows, sh_g[:, : BC + HM].astype(bf16)], 1)
    in_out = across(in_rows, dp)
    d_in, d_g_gain = rms_back(gn, own_input, g_gain, own_r_g)
    gil = (d_in + gpo_own).astype(bf16)

    taps_grad = jnp.zeros((XBC, KC), f32)
    taps_grad = lax.dynamic_update_slice(taps_grad, d_taps[:, :wn].T, (me * wn, 0))
    taps_grad = lax.dynamic_update_slice(taps_grad, d_taps[:, wn:].T, (DI, 0))
    bias_grad = jnp.zeros((XBC,), f32)
    bias_grad = lax.dynamic_update_slice(bias_grad, d_bias[:wn], (me * wn,))
    bias_grad = lax.dynamic_update_slice(bias_grad, d_bias[wn:], (DI,))
    terms = jnp.concatenate(
        [d_g_gain.reshape(n, dn), d_l_gain.reshape(n, dn), d_f_gain.reshape(n, dn),
         taps_grad.reshape(n, xn * KC), bias_grad.reshape(n, xn)], 1
    )
    terms = jnp.pad(terms, ((0, 0), (0, 1024 - terms.shape[1]))).reshape(n, 8, 128)
    gil_all, own_terms = communicate(n, 6, ("gather", gil), ("sum", terms))
    gil_all = gil_all.reshape(T, D)
    rows_n = PATCH * VOCAB // n
    j = (me * rows_n) // VOCAB
    first_row = (me * rows_n) % VOCAB
    own_ids = lax.dynamic_slice_in_dim(earlier, j, 1, 1)
    own_hot = (own_ids == first_row + jnp.arange(rows_n, dtype=jnp.int32)[None, :]).astype(bf16)
    pt_own = dot(own_hot, lax.dynamic_slice_in_dim(gil_all, j * DG, DG, 1), TN)
    rest = jnp.concatenate([own_terms.reshape(-1), d_m_gain, d_step_b, d_decay, d_skip])
    pt_out = across(pt_own, dp)
    rest = across(rest, dp)
    cut = [dn, dn, dn, xn * KC, xn, 1024 - 3 * dn - xn * (KC + 1), wn, hn, hn, hn]
    bits = []
    at = 0
    for s in cut:
        bits.append(rest[at : at + s])
        at += s
    return (
        activations,
        pt_out,
        bits[0],
        in_out,
        bits[3].reshape(xn, KC),
        bits[4],
        bits[7],
        bits[8],
        bits[9],
        bits[6],
        op_out,
        across(byte_g, dp),
        bits[1],
        across(qkv_g, dp),
        across(attn_g, dp),
        bits[2],
        gu_out,
        down_out,
    )


def solution(mesh):
    row, mat = P("fsdp"), P("fsdp", None)
    in_specs = (
        P("dp", "fsdp"), P("dp", "fsdp", None), mat, row, mat, mat, row, row, row, row, row,
        mat, mat, row, mat, mat, row, mat, mat,
    )
    out_specs = (
        P("dp", "fsdp", None), mat, row, mat, mat, row, row, row, row, row, mat, mat, row,
        mat, mat, row, mat, mat,
    )
    body = functools.partial(on_device, mesh.shape["fsdp"], mesh.shape["dp"])
    return jax.shard_map(body, mesh=mesh, in_specs=in_specs, out_specs=out_specs, check_vma=False)
```

time: 1700 us -> 609 us (0.36)
  waiting for transfers between devices: 1160 us -> 72.6 us
  Pallas kernels: 0 us -> 328 us
  blocking collectives: 224 us -> 23.2 us
  matrix products: 148 us -> 73.8 us
  other arithmetic: 82.8 us -> 40.7 us
    reduce_scatter x8 -> x3, waiting for transfers between devices: 674 us -> 63.2 us  [the longest x1 63.2 us: on_device(): qkv_g = scatter(dot(first_norm, grad_qkv_rows, TN).astype(bf16))]
    all_gather x8 -> x3, waiting for transfers between devices: 388 us -> 0.01 us  [the longest x1 0.01 us: on_device(): cot_all = gather(cotangent.reshape(L, D))]
    pallas_call x0 -> x9, Pallas kernels: none -> 328 us  [the longest x7 311 us: communicate(): pl.pallas_call(functools.partial(comm_kernel, tuple(kinds), tuple(counts)...]
    unnamed x2 -> x0, blocking collectives: 125 us -> none
    psum x2 -> x0, waiting for transfers between devices: 91.4 us -> none  [the longest x1 71.5 us: on_device(): lax.psum(owned[2].astype(jnp.bfloat16), 'dp').astype(jnp.float32)]
    all_gather x5 -> x1, blocking collectives: 98.7 us -> 23.2 us  [on_device(): byte_full = gather(byte_table)]
    dot_general x40 -> x30, matrix products: 148 us -> 73.8 us  [the longest x21 61.9 us: dot(): return lax.dot_general(a, b, (dims, ((), ())), preferred_element_type=f32)]
    convert_element_type x45 -> x5, other arithmetic: 42.9 us -> 4.38 us  [the longest x1 1.17 us: on_device(): step_bias.astype(f32)]
  transfers between devices with their start and end apart: 22 -> 15, of which waited for: 18 -> 4; matrix products, arithmetic and copies ran while one was open for 8% -> 19% of each run, Pallas kernels for 0% -> 41%
where the time goes in v1:
time: 609 us; the launch traced here: 601 us
  Pallas kernels  328 us (54%)
  matrix products  73.8 us (12%)
  waiting for transfers between devices  72.6 us (12%)
  other arithmetic  40.7 us (7%)
  local copies, waits for them, and re-layouts  35.9 us (6%)
  blocking collectives  23.2 us (4%)
  between operations  16 us (3%)
  starting transfers between devices  11.1 us (2%)
    pallas_call x7, Pallas kernels, communicate(): pl.pallas_call(functools.partial(comm_kernel, tuple(kinds), tuple(counts)...  311 us
    reduce_scatter x1, waiting for transfers between devices, on_device(): qkv_g = scatter(dot(first_norm, grad_qkv_rows, TN).astype(bf16))  63.2 us
    dot_general x21, matrix products, dot(): return lax.dot_general(a, b, (dims, ((), ())), preferred_element_type=f32)  61.9 us
    all_gather x1, blocking collectives, on_device(): byte_full = gather(byte_table)  23.2 us
  transfers between devices with their start and end apart: 15, of which 4 were waited for; matrix products, arithmetic and copies ran while one was open for 19% of the time, Pallas kernels for 41%

profile of v1, /device:TPU:0, one launch (start us, length us, event | category | flops | bytes accessed | tf_op | source)
XLA Modules:
  0.0 601.1 jit_solution(13233815138594249816)
XLA Ops:
  19.9 64.4 %comm_0.1 = (s32[16,1,128]{2,1,0:T(1,128)}, bf16[16,16,128]{2,1,0:T(8,128)(2,1)}, bf16[16,128,128]{2,1,0:T(8,128)(2,1)}, bf16[16,64,384]{2,1,0:T(8,128)(2,1)}, b...) custom-call(s32[1,128]{1,0:T(1,128)} %refs_0_.1, bf16[16,128]{1,0:T(8,128)(2,1)} %pad_bitcast_fusion.1.refs_1_, ...), custom_call_target="tpu_custom_call" | custom-call | tf_op jit(solution)/shard_map/comm_0/pallas_call | solution.py:251
  99.6 2.5 fusion.19
  106.5 37.0 %comm_1.1 = f32[16,1152]{1,0:T(8,128)} custom-call(bf16[4,2,2,16,1152]{4,3,2,1,0:T(8,128)(2,1)} %pad_maximum_fusion.4.refs_0_), custom_call_target="tpu_custom_call" | custom-call | tf_op jit(solution)/shard_map/comm_1/pallas_call | solution.py:251
  145.2 23.2 %all_gather.12 = bf16[256,1024]{1,0:T(8,128)(2,1)S(1)} all-gather(bf16[16,1024]{1,0:T(8,128)(2,1)} %param.31), channel_id=1, replica_groups=mesh['dp'=2,'fsdp'=16] {'fsdp'}, dimensions={0}, use_global_device_ids=true | all-gather | bytes 557056 | tf_op jit(solution)/shard_map/all_gather | solution.py:425
  170.0 5.0 fusion.96.qkv_ref
  174.9 7.3 %attend.1 = bf16[128,1024]{1,0:T(8,128)(2,1)} custom-call(f32[128,3072]{1,0:T(8,128)} %fusion.96.qkv_ref), custom_call_target="tpu_custom_call" | custom-call | tf_op jit(solution)/shard_map/attend/pallas_call | solution.py:313
  185.4 47.8 %comm_2.1 = bf16[16,128,1024]{2,1,0:T(8,128)(2,1)} custom-call(bf16[128,1024]{1,0:T(8,128)(2,1)} %multiply_convert_fusion.4.refs_0_), custom_call_target="tpu_custom_call" | custom-call | tf_op jit(solution)/shard_map/comm_2/pallas_call | solution.py:251
  233.2 6.8 %fusion.106 = f32[2048,512]{1,0:T(8,128)} fusion(bf16[2048,1024]{1,0:T(8,128)(2,1)} %bitcast.141, bf16[1024,512]{1,0:T(8,128)(2,1)} %bitcast.185), kind=kOutput, calls=%fused_computation.222 | convolution fusion | flops 2147483648 | bytes 9437184 | tf_op jit(solution)/shard_map/dot_general | solution.py:275
  240.0 5.4 multiply_convert_fusion.1
  245.4 3.3 convolution_convert_fusion.1
  248.8 4.4 convolution_convert_fusion.2
  253.2 8.2 %pad_maximum_fusion.refs_0_ = bf16[4,2,2,128,2048]{4,3,2,1,0:T(8,128)(2,1)} fusion(bf16[4,2,2,128,1024]{4,3,2,1,0:T(8,128)(2,1)} %convolution_convert_fusion.2, bf16[4,2,2,128,1024]{4,3,2,1,0:T(8,128)(2,1)} %bitcast.138), kind=kLoop, calls=%fused_computation | loop fusion | flops 16777216 | bytes 16777216 | tf_op jit(solution)/shard_map/concatenate | solution.py:512
  261.4 73.1 %comm_3.1 = f32[128,2048]{1,0:T(8,128)} custom-call(bf16[4,2,2,128,2048]{4,3,2,1,0:T(8,128)(2,1)} %pad_maximum_fusion.refs_0_), custom_call_target="tpu_custom_call" | custom-call | tf_op jit(solution)/shard_map/comm_3/pallas_call | solution.py:251
  340.3 9.8 %attend_back.1 = bf16[128,3072]{1,0:T(8,128)(2,1)} custom-call(f32[128,3072]{1,0:T(8,128)} %fusion.96.qkv_ref, f32[128,1024]{1,0:T(8,128)} %fusion.50.g_ref), custom_call_target="tpu_custom_call" | custom-call | tf_op jit(solution)/shard_map/attend_back/pallas_call | solution.py:348
  350.1 6.0 multiply_reduce_fusion.1
  365.5 4.5 convolution_convert_fusion
  371.4 6.4 %fusion.13 = bf16[1024,512]{1,0:T(8,128)(2,1)} fusion(bf16[2048,1024]{1,0:T(8,128)(2,1)} %bitcast.142, bf16[2048,256]{1,0:T(8,128)(2,1)} %copy-done.81, bf16[2048,256]{1,0:T(8,128)(2,1)} %copy-done.80), kind=kOutput, calls=%fused_computation.25 | convolution fusion | flops 2152202240 | bytes 7340032 | tf_op jit(solution)/shard_map/dot_general | solution.py:275
  377.8 29.4 %comm_4.1 = (bf16[16,16,1024]{2,1,0:T(8,128)(2,1)}, f32[16,16,128]{2,1,0:T(8,128)}, bf16[16,64,512]{2,1,0:T(8,128)(2,1)}) custom-call(bf16[16,1024]{1,0:T(8,128)(2,1)} %get-tuple-element.126.refs_0_, f32[16,128]{1,0:T(8,128)} %broadcast_select_fusion.refs_1_, bf16[16,64,512]{2,1,0:T(8,128)(2,1)} %bitcast.159), custom_call_target="tpu_custom_call" | custom-call | tf_op jit(solution)/shard_map/comm_4/pallas_call | solution.py:251
  408.5 2.5 multiply_reduce_fusion.11
  437.1 40.9 %comm_5.1 = (bf16[16,64,256]{2,1,0:T(8,128)(2,1)}, f32[64,384]{1,0:T(8,128)}, f32[16,1024]{1,0:T(8,128)}) custom-call(bf16[16,64,256]{2,1,0:T(8,128)(2,1)} %slice.216.refs_0_, bf16[4,2,2,64,384]{4,3,2,1,0:T(8,128)(2,1)} %bitcast.149, bf16[4,2,2,16,1024]{4,3,2,1,0:T(8,128)(2,1)} %bitcast.161), custom_call_target="tpu_custom_call" | custom-call | tf_op jit(solution)/shard_map/comm_5/pallas_call | solution.py:251
  481.9 18.0 %comm_6.1 = (bf16[16,16,1024]{2,1,0:T(8,128)(2,1)}, f32[8,128]{1,0:T(8,128)}) custom-call(bf16[16,1024]{1,0:T(8,128)(2,1)} %add_convert_fusion.1.refs_0_, f32[4,2,2,8,128]{4,3,2,1,0:T(8,128)} %bitcast.168), custom_call_target="tpu_custom_call" | custom-call | tf_op jit(solution)/shard_map/comm_6/pallas_call | solution.py:251
  519.3 63.2 %reduce-scatter.6.cloned.1.call-done = bf16[64,3072]{1,0:T(8,128)(2,1)} async-done(((bf16[1024,3072]{1,0:T(8,128)(2,1)}), bf16[64,3072]{1,0:T(8,128)(2,1)}) %reduce-scatter.6.cloned.1.call-update) | async-done | bytes 393232 | tf_op jit(solution)/shard_map/reduce_scatter | solution.py:529
  583.9 2.8 convert_add_fusion
  587.5 5.3 collective-permute-done.5
  (367 shorter events, 107.6 us)
Async XLA Ops:
  7.2 232.8 %copy-start = (bf16[256,1024]{1,0:T(8,128)(2,1)S(1)}, bf16[256,1024]{1,0:T(8,128)(2,1)}, u32[]{:S(2)}) copy-start(bf16[256,1024]{1,0:T(8,128)(2,1)} %param.37) | copy-start | bytes 1572868
  7.2 162.8 %all-gather.5.cloned.1.call-start = ((), (), s32[]{:S(2)}) async-start(), calls=%async_computation.3 | async-start | bytes 6684672 | tf_op jit(solution)/shard_map/all_gather | solution.py:424
  7.9 174.4 %all-gather.7.cloned.1.call-start = ((), (), s32[]{:S(2)}) async-start(), calls=%async_computation.4 | async-start | bytes 2228224 | tf_op jit(solution)/shard_map/all_gather | solution.py:426
  8.7 231.3 %all-gather.9.cloned.1.call-start = ((), (), s32[]{:S(2)}) async-start(), calls=%async_computation.8 | async-start | bytes 4456448 | tf_op jit(solution)/shard_map/all_gather | solution.py:427
  9.4 503.0 %reduce-scatter.4.cloned.1.call-start = ((), (), s32[]{:S(2)}) async-start(), calls=%async_computation.5 | async-start | bytes 557056 | tf_op jit(solution)/shard_map/reduce_scatter | solution.py:533
  103.1 66.3 %copy-start.21 = (f32[256,128]{1,0:T(8,128)}, f32[256,128]{1,0:T(8,128)S(1)}, u32[]{:S(2)}) copy-start(f32[256,128]{1,0:T(8,128)S(1)} %copy.116) | copy-start | bytes 393220
  103.8 65.6 %copy-start.12 = (f32[256,128]{1,0:T(8,128)}, f32[256,128]{1,0:T(8,128)S(1)}, u32[]{:S(2)}) copy-start(f32[256,128]{1,0:T(8,128)S(1)} %get-tuple-element.130) | copy-start | bytes 393220
  170.0 180.1 %copy-start.43 = (f32[128]{0:T(128)}, f32[128]{0:T(128)S(1)}, u32[]{:S(2)}) copy-start(f32[128]{0:T(128)S(1)} %get-tuple-element.159) | copy-start | bytes 1540
  261.4 75.1 %copy-start.17 = (bf16[1,128,1024]{2,1,0:T(8,128)(2,1)S(1)}, bf16[1,128,1024]{2,1,0:T(8,128)(2,1)}, u32[]{:S(2)}) copy-start(bf16[1,128,1024]{2,1,0:T(8,128)(2,1)} %param.20) | copy-start | bytes 786436
  359.0 158.7 %reduce-scatter.8.cloned.1.call-start = ((), (), s32[]{:S(2)}) async-start(), calls=%async_computation.7 | async-start | bytes 2228224 | tf_op jit(solution)/shard_map/reduce_scatter | solution.py:526
  361.2 221.3 %reduce-scatter.6.cloned.1.call-start = ((), (), s32[]{:S(2)}) async-start(), calls=%async_computation.6 | async-start | bytes 6684672 | tf_op jit(solution)/shard_map/reduce_scatter | solution.py:529
  371.4 37.2 %copy-start.25 = (bf16[128,1024]{1,0:T(8,128)(2,1)S(1)}, bf16[128,1024]{1,0:T(8,128)(2,1)}, u32[]{:S(2)}) copy-start(bf16[128,1024]{1,0:T(8,128)(2,1)} %param.30) | copy-start | bytes 786436
  371.4 37.2 %copy-start.57 = (f32[128]{0:T(128)S(1)}, f32[128]{0:T(128)}, u32[]{:S(2)}) copy-start(f32[128]{0:T(128)} %convert_element_type.147) | copy-start | bytes 1540
  426.9 83.2 %collective-permute-start.8 = (bf16[256,1024]{1,0:T(8,128)(2,1)}, bf16[256,1024]{1,0:T(8,128)(2,1)}, u32[]{:S(2)}, u32[]{:S(2)}) collective-permute-start(bf16[256,1024]{1,0:T(8,128)(2,1)} %fusion.16), channel_id=1, source_target_pairs={{0,16},{16,0},{1,17},{17,1},{2,18},{18,2},{3,19},{19,3},{4,20},{20... | collective-permute-start | bytes 1572872 | tf_op jit(solution)/shard_map/ppermute | solution.py:388
  430.4 77.8 %collective-permute-start.3 = (bf16[128,1024]{1,0:T(8,128)(2,1)S(1)}, bf16[128,1024]{1,0:T(8,128)(2,1)}, u32[]{:S(2)}, u32[]{:S(2)}) collective-permute-start(bf16[128,1024]{1,0:T(8,128)(2,1)S(1)} %convolution_convert_fusion.8), channel_id=1, source_target_pairs={{0,16},{16,0},{1,17},{17,1},{2,18},{18,2},{3,19},{19,3},{4,20},{20... | collective-permute-start | bytes 786440 | tf_op jit(solution)/shard_map/ppermute | solution.py:388
  434.3 149.7 %collective-permute-start.7 = (bf16[64,8192]{1,0:T(8,128)(2,1)S(1)}, bf16[64,8192]{1,0:T(8,128)(2,1)}, u32[]{:S(2)}, u32[]{:S(2)}) collective-permute-start(bf16[64,8192]{1,0:T(8,128)(2,1)S(1)} %bitcast.147), channel_id=1, source_target_pairs={{0,16},{16,0},{1,17},{17,1},{2,18},{18,2},{3,19},{19,3},{4,20},{20... | collective-permute-start | bytes 3145736 | tf_op jit(solution)/shard_map/ppermute | solution.py:388
  437.1 43.1 %copy-start.53 = (f32[16]{0:T(128)S(1)}, f32[16]{0:T(128)}, u32[]{:S(2)}) copy-start(f32[16]{0:T(128)} %get-tuple-element.124) | copy-start | bytes 196
  500.7 3.7 collective-permute-start.1
  501.9 5.7 collective-permute-start
  504.4 11.5 %collective-permute-start.2 = (bf16[64,4384]{1,0:T(8,128)(2,1)S(1)}, bf16[64,4384]{1,0:T(8,128)(2,1)S(1)}, u32[]{:S(2)}, u32[]{:S(2)}) collective-permute-start(bf16[64,4384]{1,0:T(8,128)(2,1)S(1)} %pad_maximum_fusion.5), channel_id=1, source_target_pairs={{0,16},{16,0},{1,17},{17,1},{2,18},{18,2},{3,19},{19,3},{4,20},{20... | collective-permute-start | bytes 1683464 | tf_op jit(solution)/shard_map/ppermute | solution.py:388
  512.4 4.6 collective-permute-start.4
  517.7 69.0 %copy-start.32 = (bf16[64,1024]{1,0:T(8,128)(2,1)S(1)}, bf16[64,1024]{1,0:T(8,128)(2,1)}, u32[]{:S(2)}) copy-start(bf16[64,1024]{1,0:T(8,128)(2,1)} %reduce-scatter.8.cloned.1.call-done) | copy-start | bytes 393220
  517.7 69.0 %collective-permute-start.6 = (bf16[64,1024]{1,0:T(8,128)(2,1)}, bf16[64,1024]{1,0:T(8,128)(2,1)S(1)}, u32[]{:S(2)}, u32[]{:S(2)}) collective-permute-start(bf16[64,1024]{1,0:T(8,128)(2,1)} %reduce-scatter.8.cloned.1.call-done), channel_id=1, source_target_pairs={{0,16},{16,0},{1,17},{17,1},{2,18},{18,2},{3,19},{19,3},{4,20},{20... | collective-permute-start | bytes 393224 | tf_op jit(solution)/shard_map/ppermute | solution.py:388
  582.5 10.4 %collective-permute-start.5 = (bf16[64,3072]{1,0:T(8,128)(2,1)}, bf16[64,3072]{1,0:T(8,128)(2,1)S(1)}, u32[]{:S(2)}, u32[]{:S(2)}) collective-permute-start(bf16[64,3072]{1,0:T(8,128)(2,1)} %reduce-scatter.6.cloned.1.call-done), channel_id=1, source_target_pairs={{0,16},{16,0},{1,17},{17,1},{2,18},{18,2},{3,19},{19,3},{4,20},{20... | collective-permute-start | bytes 1179656 | tf_op jit(solution)/shard_map/ppermute | solution.py:388
  (78 other events, 630.2 us)
Sparse Core Ops, SparseCore 0:
  10.3 93.2 all-gather.4
  105.8 44.8 all-gather.6
  152.8 63.9 all-gather.8
  359.1 66.1 reduce-scatter.3
  429.5 64.8 reduce-scatter.7
  498.2 84.2 reduce-scatter.5
